TPU v7x, 32 devices: a whole 2x2x4 slice. The times are simulated.
32 devices in a mesh: dom: 8 (over y, x, core), col: 4 (over z).
Axes of the slice: x: 2, y: 2, z: 4, core: 2. Of those that a mesh axis runs over, the one named last changes fastest.
Arguments:
- features: bfloat16 [65536, 1024], P('dom', 'col')
- weight: bfloat16 [1024, 1024], P(None, 'col'), may hold values from -0.1875 to 0.1875
- out_bias: bfloat16 [1024], P('col'), may hold values from -3 to 3
- local_index: int32 [8, 64, 4], P('dom'), may hold values from 0 to 63
- local_count: int32 [8, 64], P('dom'), may hold values from 1 to 4, as said below
- local_vals: bfloat16 [8, 64, 4, 128, 128], P('dom'), may hold values from -0.1875 to 0.1875
- halo_index: int32 [8, 64, 4], P('dom'), may hold values from 0 to 31
- halo_count: int32 [8, 64], P('dom'), may hold values from 0 to 4, as said below
- halo_vals: bfloat16 [8, 64, 4, 128, 128], P('dom'), may hold values from -0.1875 to 0.1875
- send_rows: int32 [8, 8, 512], P('dom'), may hold values from 0 to 8191
- send_count: int32 [8, 8], P('dom'), may hold values from 0 to 512, as said below
Outputs:
- normalized: bfloat16 [65536, 1024], P('dom', 'col')
- channel_stats: float32 [2, 1024], P(None, 'col')
Inputs may be any that keep to these rules, and one draw needn't show every extreme that they name: `local_index`: slots k >= local_count of a row tile are not used. `local_count`: every partition has a row tile with all 4 slots used. `halo_index`: slots k >= halo_count of a row tile are not used. `halo_count`: every partition has a row tile with all 4 slots used. `send_rows`: slots s >= send_count[q, p] are not used. send_count[p, p] is 0; every partition fills all 512 slots to some other partition.
All inputs are finite; a program needn't handle non-finite values.
Results may differ from a plain program's by a relative error of at most 0.0075.
Values may be sent and summed in bfloat16 or wider, within the bound.
A program may use at most 192 MiB of HBM per device.

v0:
```python
import jax
import jax.numpy as jnp
from jax import lax
from jax.sharding import PartitionSpec as P

TILE = 128
epsilon = 1e-06


def tile_sum(sources, tile_index, tile_count, tile_vals):
    gathered = sources[tile_index]
    keep_mask = jnp.arange(tile_vals.shape[1])[None, :] < tile_count[:, None]
    masked = jnp.where(keep_mask[:, :, None, None], tile_vals, jnp.zeros_like(tile_vals))
    return jnp.einsum("tkij,tkjc->tic", masked, gathered, preferred_element_type=jnp.float32)


def on_device(
    features,
    weight,
    out_bias,
    local_index,
    local_count,
    local_vals,
    halo_index,
    halo_count,
    halo_vals,
    send_rows,
    send_count,
):
    row_count, col_width = features.shape
    peer_count = lax.axis_size("dom")
    slot_total = send_rows.shape[2]
    chosen = features[send_rows[0]]
    keep_mask = jnp.arange(slot_total)[None, :] < send_count[0][:, None]
    outgoing = jnp.where(keep_mask[:, :, None], chosen, jnp.zeros_like(chosen))
    arrived = lax.all_to_all(outgoing, "dom", split_axis=0, concat_axis=0, tiled=True)
    halo_tiles = arrived.reshape(peer_count * slot_total // TILE, TILE, col_width)
    own_tiles = features.reshape(row_count // TILE, TILE, col_width)
    summed = tile_sum(own_tiles, local_index[0], local_count[0], local_vals[0])
    summed = summed + tile_sum(halo_tiles, halo_index[0], halo_count[0], halo_vals[0])
    spread = summed.reshape(row_count, col_width).astype(jnp.bfloat16)
    node_total = row_count * peer_count
    regrouped = lax.all_to_all(spread, "col", split_axis=0, concat_axis=1, tiled=True)
    full_weight, full_bias = (
        lax.all_gather(weight, "col", axis=1, tiled=True),
        lax.all_gather(out_bias.reshape(1, col_width), "col", axis=1, tiled=True),
    )
    mixed_rows = jnp.dot(regrouped, full_weight, preferred_element_type=jnp.float32) + full_bias[
        0
    ].astype(jnp.float32)
    active = jnp.maximum(mixed_rows, 0.0)
    row_power = jnp.mean(active * active, axis=1, keepdims=True)
    scaled = active * lax.rsqrt(row_power + epsilon)
    sum_whole, square_whole = lax.psum(
        (jnp.sum(scaled, axis=0), jnp.sum(scaled * scaled, axis=0)), ("dom", "col")
    )
    normalized = lax.all_to_all(
        scaled.astype(jnp.bfloat16), "col", split_axis=1, concat_axis=0, tiled=True
    )
    column_start = lax.axis_index("col") * col_width
    sum_total = lax.dynamic_slice_in_dim(sum_whole, column_start, col_width, 0)
    square_total = lax.dynamic_slice_in_dim(square_whole, column_start, col_width, 0)
    channel_mean = sum_total / node_total
    channel_var = square_total / node_total - channel_mean * channel_mean
    return (normalized, jnp.stack([channel_mean, channel_var]))


def solution(mesh):
    in_specs = (
        P("dom", "col"),
        P(None, "col"),
        P("col"),
        P("dom", None, None),
        P("dom", None),
        P("dom", None, None, None, None),
        P("dom", None, None),
        P("dom", None),
        P("dom", None, None, None, None),
        P("dom", None, None),
        P("dom", None),
    )
    out_specs = (P("dom", "col"), P(None, "col"))
    return jax.shard_map(
        on_device, mesh=mesh, in_specs=in_specs, out_specs=out_specs, check_vma=False
    )
```

profile of v0, /device:TPU:0, one launch (start us, length us, event | category | flops | bytes accessed | tf_op | source)
XLA Modules:
  0.0 374.6 jit_solution(2426596609186330712)
XLA Ops:
  7.2 0.7 fusion.10
  7.9 0.7 iota_compare_fusion.2
  8.6 15.7 %gather_fusion.1 = bf16[4096,256]{1,0:T(8,128)(2,1)S(1)} fusion(bf16[8192,256]{1,0:T(8,128)(2,1)} %param.11, s32[4096]{0:T(1024)S(1)} %broadcast_clamp_fusion), kind=kCustom, calls=%fused_computation.1 | custom fusion | bytes 4210688 | tf_op jit(solution)/shard_map/gather | solution.py:33
  24.4 0.0 copy-start
  24.4 0.0 copy-start.1
  24.4 1.7 broadcast_select_fusion
  26.1 5.2 %all-to-all-start = ((bf16[8,512,256]{2,1,0:T(8,128)(2,1)}), bf16[8,512,256]{2,1,0:T(8,128)(2,1)S(1)}, u32[]{:S(2)}, u32[]{:S(2)}) async-start(bf16[8,512,256]{2,1,0:T(8,128)(2,1)} %broadcast_select_fusion), calls=%async_computation | async-start | bytes 4194304 | tf_op jit(solution)/shard_map/all_to_all | solution.py:36
  31.3 0.0 copy-done
  31.3 0.1 copy.19
  31.4 0.1 reshape.208
  31.5 0.0 copy-done.1
  31.5 0.1 copy.18
  31.6 0.1 reshape.192
  31.7 0.0 copy-start.2
  31.7 0.0 copy-start.3
  31.7 12.0 %gather_fusion = bf16[256,128,256]{2,1,0:T(8,128)(2,1)} fusion(bf16[64,128,256]{2,1,0:T(8,128)(2,1)} %bitcast.52, s32[1024]{0:T(1024)S(1)} %pad_clamp_fusion.1), kind=kCustom, calls=%fused_computation | custom fusion | bytes 33555456 | tf_op jit(solution)/shard_map/gather | solution.py:11
  43.7 0.0 copy-done.2
  43.7 0.1 iota_compare_fusion
  43.8 0.0 copy-done.3
  43.8 0.1 iota_compare_fusion.1
  43.9 14.0 %all-to-all-done = bf16[8,512,256]{2,1,0:T(8,128)(2,1)S(1)} async-done(((bf16[8,512,256]{2,1,0:T(8,128)(2,1)}), bf16[8,512,256]{2,1,0:T(8,128)(2,1)S(1)}, u32[]{:S(2)}, u32[]{:S(2)}) %all-to-all-start) | async-done | bytes 2097184 | tf_op jit(solution)/shard_map/all_to_all | solution.py:36
  57.9 9.7 %gather_fusion.2 = bf16[256,128,256]{2,1,0:T(8,128)(2,1)} fusion(bf16[32,128,256]{2,1,0:T(8,128)(2,1)S(1)} %bitcast.53, s32[1024]{0:T(1024)S(1)} %pad_clamp_fusion), kind=kCustom, calls=%fused_computation.2 | custom fusion | bytes 33555456 | tf_op jit(solution)/shard_map/gather | solution.py:11
  67.6 13.8 %fusion.1 = f32[64,128,256,1]{2,1,3,0:T(8,128)} fusion(bf16[64,4,128,256]{3,2,1,0:T(8,128)(2,1)} %bitcast.54, bf16[1,64,4,128,128]{4,3,2,1,0:T(8,128)(2,1)} %param.19, pred[64,4]{1,0:T(8,128)(4,1)S(1)} %iota_compare_fusion), kind=kOutput, calls=%fused_computation.6 | convolution fusion | flops 2151677952 | bytes 33554688 | tf_op jit(solution)/shard_map/tkij,tkjc->tic/dot_general | solution.py:14
  81.4 14.0 %fusion = bf16[64,128,256]{2,1,0:T(8,128)(2,1)} fusion(f32[64,128,256,1]{2,1,3,0:T(8,128)} %fusion.1, bf16[64,4,128,256]{3,2,1,0:T(8,128)(2,1)} %bitcast.55, bf16[1,64,4,128,128]{4,3,2,1,0:T(8,128)(2,1)} %param.16, pred[64,4]{1,0:T(8,128)(4,1)S(1)} %iota_compare_fusion.1), kind=kOutput, calls=%fused_computation.4 | convolution fusion | flops 2155872256 | bytes 37748992 | tf_op jit(solution)/shard_map/tkij,tkjc->tic/dot_general | solution.py:14
  95.4 0.0 copy-start.4
  95.4 6.3 %copy.20 = bf16[4,2048,256]{1,2,0:T(8,128)(2,1)} copy(bf16[4,2048,256]{2,1,0:T(8,128)(2,1)} %bitcast.56) | data formatting | bytes 8388608 | tf_op jit(solution)/shard_map/convert_element_type | solution.py:41
  101.6 4.9 %all-to-all-start.1 = ((bf16[4,2048,256]{1,2,0:T(8,128)(2,1)}), bf16[4,2048,256]{1,2,0:T(8,128)(2,1)}, u32[]{:S(2)}, u32[]{:S(2)}) async-start(bf16[4,2048,256]{1,2,0:T(8,128)(2,1)} %copy.20), calls=%async_computation.1 | async-start | bytes 8388608 | tf_op jit(solution)/shard_map/all_to_all | solution.py:43
  106.5 0.0 all-gather.4.cloned.1.call-start
  106.5 0.7 all-gather.4.cloned.1.call-update
  107.2 0.0 copy-done.4
  107.3 103.9 %all-gather.1 = bf16[4,1,256]{2,1,0:T(2,128)(2,1)S(1)} all-gather(bf16[1,1,256]{2,1,0:T(2,128)(2,1)S(1)} %reshape.220), channel_id=2, replica_groups=mesh['dom'=8,'col'=4] {'col'}, dimensions={0}, use_global_device_ids=true | all-gather | bytes 2560 | tf_op jit(solution)/shard_map/all_gather | solution.py:46
  211.2 0.0 all-gather.4.cloned.1.call-done
  211.2 19.8 %all-to-all-done.1 = bf16[4,2048,256]{1,2,0:T(8,128)(2,1)} async-done(((bf16[4,2048,256]{1,2,0:T(8,128)(2,1)}), bf16[4,2048,256]{1,2,0:T(8,128)(2,1)}, u32[]{:S(2)}, u32[]{:S(2)}) %all-to-all-start.1) | async-done | bytes 4194336 | tf_op jit(solution)/shard_map/all_to_all | solution.py:43
  231.0 7.8 %multiply_reduce_fusion.1 = (f32[2048]{0:T(1024)S(1)}, f32[2048,1024]{0,1:T(8,128)S(1)}) fusion(f32[1024]{0:T(1024)S(1)} %bitcast.61, bf16[2048,1024]{0,1:T(8,128)(2,1)} %bitcast.19, bf16[1024,1024]{1,0:T(8,128)(2,1)} %all-gather.4.cloned.1.call-done), kind=kOutput, calls=%fused_computation.10 | convolution fusion | flops 4303353856 | bytes 14692352 | tf_op jit(solution)/shard_map/dot_general | solution.py:48
  238.8 3.5 fusion.6
  242.2 4.8 %all-to-all-start.2 = ((bf16[2048,4,256]{0,2,1:T(8,128)(2,1)}), bf16[2048,4,256]{0,2,1:T(8,128)(2,1)}, u32[]{:S(2)}, u32[]{:S(2)}) async-start(bf16[2048,4,256]{0,2,1:T(8,128)(2,1)} %bitcast.57), calls=%async_computation.2 | async-start | bytes 8388608 | tf_op jit(solution)/shard_map/all_to_all | solution.py:57
  247.1 113.8 %all-reduce = (f32[1024]{0:T(1024)S(1)}, f32[1024]{0:T(1024)S(1)}) all-reduce(f32[1024]{0:T(1024)S(1)} %get-tuple-element.3, f32[1024]{0:T(1024)S(1)} %get-tuple-element.2), channel_id=1, replica_groups=mesh['dom'=8,'col'=4] {'dom','col'}, use_global_device_ids=true, to_apply=%region_4.5 | all-reduce | flops 2048 | bytes 16384 | tf_op jit(solution)/shard_map/psum | solution.py:54
  360.9 0.1 dynamic-slice_multiply_fusion
  361.0 0.6 pad_maximum_fusion
  361.5 0.0 all-to-all-done.2
  361.6 6.2 %copy.21 = bf16[4,2048,256]{2,1,0:T(8,128)(2,1)} copy(bf16[4,2048,256]{1,2,0:T(8,128)(2,1)} %bitcast.22) | data formatting | bytes 8388608 | tf_op jit(solution)/shard_map/all_to_all | solution.py:57
  (9 shorter events, 0.1 us)
Async XLA Ops:
  24.4 6.9 %copy-start = (s32[1,64,4]{1,2,0:T(4,128)S(1)}, s32[1,64,4]{1,2,0:T(4,128)}, u32[]{:S(2)}) copy-start(s32[1,64,4]{1,2,0:T(4,128)} %param.17) | copy-start | bytes 3076
  24.4 7.1 %copy-start.1 = (s32[1,64,4]{1,2,0:T(4,128)S(1)}, s32[1,64,4]{1,2,0:T(4,128)}, u32[]{:S(2)}) copy-start(s32[1,64,4]{1,2,0:T(4,128)} %param.14) | copy-start | bytes 3076
  26.1 31.8 %all-to-all-start = ((bf16[8,512,256]{2,1,0:T(8,128)(2,1)}), bf16[8,512,256]{2,1,0:T(8,128)(2,1)S(1)}, u32[]{:S(2)}, u32[]{:S(2)}) async-start(bf16[8,512,256]{2,1,0:T(8,128)(2,1)} %broadcast_select_fusion), calls=%async_computation | async-start | bytes 4194304 | tf_op jit(solution)/shard_map/all_to_all | solution.py:36
  31.7 12.0 %copy-start.2 = (s32[1,64]{1,0:T(1,128)S(1)}, s32[1,64]{1,0:T(1,128)}, u32[]{:S(2)}) copy-start(s32[1,64]{1,0:T(1,128)} %param.18) | copy-start | bytes 772
  31.7 12.1 %copy-start.3 = (s32[1,64]{1,0:T(1,128)S(1)}, s32[1,64]{1,0:T(1,128)}, u32[]{:S(2)}) copy-start(s32[1,64]{1,0:T(1,128)} %param.15) | copy-start | bytes 772
  95.4 11.9 %copy-start.4 = (bf16[256]{0:T(256)(128)(2,1)S(1)}, bf16[256]{0:T(256)(128)(2,1)}, u32[]{:S(2)}) copy-start(bf16[256]{0:T(256)(128)(2,1)} %param.13) | copy-start | bytes 1540
  101.6 129.3 %all-to-all-start.1 = ((bf16[4,2048,256]{1,2,0:T(8,128)(2,1)}), bf16[4,2048,256]{1,2,0:T(8,128)(2,1)}, u32[]{:S(2)}, u32[]{:S(2)}) async-start(bf16[4,2048,256]{1,2,0:T(8,128)(2,1)} %copy.20), calls=%async_computation.1 | async-start | bytes 8388608 | tf_op jit(solution)/shard_map/all_to_all | solution.py:43
  106.5 104.7 %all-gather.4.cloned.1.call-start = ((), (), s32[]{:S(2)}) async-start(), calls=%async_computation.3 | async-start | bytes 2621440 | tf_op jit(solution)/shard_map/all_gather | solution.py:45
  242.2 119.3 %all-to-all-start.2 = ((bf16[2048,4,256]{0,2,1:T(8,128)(2,1)}), bf16[2048,4,256]{0,2,1:T(8,128)(2,1)}, u32[]{:S(2)}, u32[]{:S(2)}) async-start(bf16[2048,4,256]{0,2,1:T(8,128)(2,1)} %bitcast.57), calls=%async_computation.2 | async-start | bytes 8388608 | tf_op jit(solution)/shard_map/all_to_all | solution.py:57
Sparse Core Ops, SparseCore 0:
  108.9 94.7 all-gather.3
where the time goes:
time: 375 us
  blocking collectives  218 us (58%)
  local copies, waits for them, and re-layouts  50.3 us (13%)
  matrix products  35.5 us (9%)
  waiting for transfers between devices  34.5 us (9%)
  starting transfers between devices  14.9 us (4%)
  between operations  14.2 us (4%)
  other arithmetic  7.48 us (2%)
    psum x1, blocking collectives, on_device(): lax.psum((jnp.sum(scaled, axis=0), jnp.sum(scaled * scaled, axis=0)), ('d...  114 us
    all_gather x1, blocking collectives, on_device(): lax.all_gather(out_bias.reshape(1, col_width), 'col', axis=1, tiled=True)  104 us
    dot_general x2, matrix products, tile_sum(): jnp.einsum('tkij,tkjc->tic', masked, gathered, preferred_element_type=jnp...  27.7 us
    gather x2, local copies, waits for them, and re-layouts, tile_sum(): gathered = sources[tile_index]  21.7 us
    all_to_all x1, waiting for transfers between devices, on_device(): lax.all_to_all(spread, 'col', split_axis=0, concat_axis=1, tiled=True)  19.8 us
    gather x1, local copies, waits for them, and re-layouts, on_device(): chosen = features[send_rows[0]]  15.7 us
    all_to_all x1, waiting for transfers between devices, on_device(): lax.all_to_all(outgoing, 'dom', split_axis=0, concat_axis=0, tiled=True)  14 us
    dot_general x1, matrix products, on_device(): jnp.dot(regrouped, full_weight, preferred_element_type=jnp.float32)  7.76 us
  transfers between devices with their start and end apart: 4, of which 2 were waited for; matrix products, arithmetic and copies ran while one was open for 4% of the time, Pallas kernels for 0%

commit v1 on v0

--- a/solution.py
+++ b/solution.py
@@ -5,6 +5,17 @@
 
 TILE = 128
 epsilon = 1e-06
+
+
+def cut_along(shard, dim, size):
+    before, after = (shard.shape[:dim], shard.shape[dim + 1 :])
+    return jnp.moveaxis(shard.reshape(*before, size, -1, *after), dim, 0)
+
+
+def joined_along(pieces, dim):
+    shape = list(pieces.shape[1:])
+    shape[dim] *= pieces.shape[0]
+    return jnp.moveaxis(pieces, 0, dim).reshape(shape)
 
 
 def tile_sum(sources, tile_index, tile_count, tile_vals):
@@ -33,7 +44,14 @@
     chosen = features[send_rows[0]]
     keep_mask = jnp.arange(slot_total)[None, :] < send_count[0][:, None]
     outgoing = jnp.where(keep_mask[:, :, None], chosen, jnp.zeros_like(chosen))
-    arrived = lax.all_to_all(outgoing, "dom", split_axis=0, concat_axis=0, tiled=True)
+    size, mine = (lax.axis_size("dom"), lax.axis_index("dom"))
+    parts = cut_along(outgoing, 0, size)
+    outs = [parts[mine]]
+    for step in range(1, size):
+        sent = parts[(mine + step) % size]
+        outs.append(lax.ppermute(sent, "dom", [(i, (i + step) % size) for i in range(size)]))
+    parts = jnp.stack(outs)[(mine - jnp.arange(size)) % size]
+    arrived = joined_along(parts, 0)
     halo_tiles = arrived.reshape(peer_count * slot_total // TILE, TILE, col_width)
     own_tiles = features.reshape(row_count // TILE, TILE, col_width)
     summed = tile_sum(own_tiles, local_index[0], local_count[0], local_vals[0])

time: 375 us -> 386 us (1.029)
  local copies, waits for them, and re-layouts: 50.3 us -> 59.2 us
  waiting for transfers between devices: 34.5 us -> 27.8 us
  starting transfers between devices: 14.9 us -> 19.7 us
    all_to_all x1 -> x0, waiting for transfers between devices: 14 us -> none  [on_device(): lax.all_to_all(outgoing, 'dom', split_axis=0, concat_axis=0, tiled=True)]
    ppermute x0 -> x7, starting transfers between devices: none -> 9.8 us  [on_device(): lax.ppermute(sent, 'dom', [(i, (i + step) % size) for i in range(size)])]
    ppermute x0 -> x7, waiting for transfers between devices: none -> 7.25 us  [on_device(): lax.ppermute(sent, 'dom', [(i, (i + step) % size) for i in range(size)])]
    all_to_all x1 -> x0, starting transfers between devices: 5.2 us -> none  [on_device(): lax.all_to_all(outgoing, 'dom', split_axis=0, concat_axis=0, tiled=True)]
  transfers between devices with their start and end apart: 4 -> 10, of which waited for: 2 -> 4; matrix products, arithmetic and copies ran while one was open for 4% -> 4% of each run, Pallas kernels for 0% -> 0%
where the time goes in v1:
time: 386 us; the launch traced here: 385 us
  blocking collectives  221 us (57%)
  local copies, waits for them, and re-layouts  59.2 us (15%)
  matrix products  35.5 us (9%)
  waiting for transfers between devices  27.8 us (7%)
  starting transfers between devices  19.7 us (5%)
  between operations  14.3 us (4%)
  other arithmetic  7.8 us (2%)
    psum x1, blocking collectives, on_device(): lax.psum((jnp.sum(scaled, axis=0), jnp.sum(scaled * scaled, axis=0)), ('d...  113 us
    all_gather x1, blocking collectives, on_device(): lax.all_gather(out_bias.reshape(1, col_width), 'col', axis=1, tiled=True)  108 us
    dot_general x2, matrix products, tile_sum(): jnp.einsum('tkij,tkjc->tic', masked, gathered, preferred_element_type=jnp...  27.7 us
    gather x2, local copies, waits for them, and re-layouts, tile_sum(): gathered = sources[tile_index]  21.9 us
    all_to_all x1, waiting for transfers between devices, on_device(): lax.all_to_all(spread, 'col', split_axis=0, concat_axis=1, tiled=True)  19.8 us
    gather x1, local copies, waits for them, and re-layouts, on_device(): chosen = features[send_rows[0]]  18.7 us
    ppermute x7, starting transfers between devices, on_device(): lax.ppermute(sent, 'dom', [(i, (i + step) % size) for i in range(size)])  9.8 us
    dot_general x1, matrix products, on_device(): jnp.dot(regrouped, full_weight, preferred_element_type=jnp.float32)  7.76 us
  transfers between devices with their start and end apart: 10, of which 4 were waited for; matrix products, arithmetic and copies ran while one was open for 4% of the time, Pallas kernels for 0%

profile of v1, /device:TPU:0, one launch (start us, length us, event | category | flops | bytes accessed | tf_op | source)
XLA Modules:
  0.0 384.9 jit_solution(8078427719252142260)
XLA Ops:
  7.3 0.7 fusion.10
  8.0 0.7 iota_compare_fusion.2
  8.7 18.7 %gather_fusion.1 = bf16[4096,256]{1,0:T(8,128)(2,1)} fusion(bf16[8192,256]{1,0:T(8,128)(2,1)} %param.11, s32[4096]{0:T(1024)S(1)} %broadcast_clamp_fusion), kind=kCustom, calls=%fused_computation.1 | custom fusion | bytes 4210688 | tf_op jit(solution)/shard_map/gather | solution.py:44
  27.4 2.0 broadcast_select_fusion
  29.4 1.3 constant_dynamic-slice_fusion
  30.7 0.5 collective-permute-start
  31.2 2.5 collective-permute-start.1
  33.7 2.4 collective-permute-start.2
  36.1 0.5 collective-permute-start.3
  36.6 0.1 collective-permute-start.4
  36.7 0.0 copy-done.2
  36.7 0.1 copy.18
  36.8 0.1 reshape.253
  36.9 0.1 copy.19
  37.0 0.1 reshape.279
  37.1 0.1 iota_compare_fusion
  37.2 0.1 iota_compare_fusion.1
  37.3 0.7 bitcast_dynamic-update-slice_fusion.7
  38.0 12.1 %gather_fusion = bf16[256,128,256]{2,1,0:T(8,128)(2,1)} fusion(bf16[64,128,256]{2,1,0:T(8,128)(2,1)} %bitcast.71, s32[1024]{0:T(1024)S(1)} %get-tuple-element.19), kind=kCustom, calls=%fused_computation | custom fusion | bytes 33555456 | tf_op jit(solution)/shard_map/gather | solution.py:22
  50.1 0.0 collective-permute-done
  50.1 1.4 collective-permute-start.5
  51.6 0.0 collective-permute-done.1
  51.6 2.4 collective-permute-start.6
  54.0 0.0 collective-permute-done.2
  54.1 0.0 collective-permute-done.3
  54.1 3.8 collective-permute-done.4
  57.9 1.3 collective-permute-done.5
  59.2 2.2 collective-permute-done.6
  61.4 0.0 copy-start.1
  61.4 1.3 copy-done.1
  62.7 2.3 gather_fusion.2
  65.0 9.7 %gather_fusion.3 = bf16[256,128,256]{2,1,0:T(8,128)(2,1)} fusion(bf16[32,128,256]{2,1,0:T(8,128)(2,1)S(1)} %bitcast.72, s32[1024]{0:T(1024)S(1)} %get-tuple-element.18), kind=kCustom, calls=%fused_computation.3 | custom fusion | bytes 33555456 | tf_op jit(solution)/shard_map/gather | solution.py:22
  74.8 13.8 %fusion.1 = f32[64,128,256,1]{2,1,3,0:T(8,128)} fusion(bf16[64,4,128,256]{3,2,1,0:T(8,128)(2,1)} %bitcast.73, bf16[1,64,4,128,128]{4,3,2,1,0:T(8,128)(2,1)} %param.19, pred[64,4]{1,0:T(8,128)(4,1)S(1)} %iota_compare_fusion), kind=kOutput, calls=%fused_computation.7 | convolution fusion | flops 2151677952 | bytes 33554688 | tf_op jit(solution)/shard_map/tkij,tkjc->tic/dot_general | solution.py:25
  88.5 14.0 %fusion = bf16[64,128,256]{2,1,0:T(8,128)(2,1)} fusion(f32[64,128,256,1]{2,1,3,0:T(8,128)} %fusion.1, bf16[64,4,128,256]{3,2,1,0:T(8,128)(2,1)} %bitcast.74, bf16[1,64,4,128,128]{4,3,2,1,0:T(8,128)(2,1)} %param.16, pred[64,4]{1,0:T(8,128)(4,1)S(1)} %iota_compare_fusion.1), kind=kOutput, calls=%fused_computation.5 | convolution fusion | flops 2155872256 | bytes 37748992 | tf_op jit(solution)/shard_map/tkij,tkjc->tic/dot_general | solution.py:25
  102.5 6.3 %copy.20 = bf16[4,2048,256]{1,2,0:T(8,128)(2,1)} copy(bf16[4,2048,256]{2,1,0:T(8,128)(2,1)} %bitcast.75) | data formatting | bytes 8388608 | tf_op jit(solution)/shard_map/convert_element_type | solution.py:59
  108.8 5.0 %all-to-all-start = ((bf16[4,2048,256]{1,2,0:T(8,128)(2,1)}), bf16[4,2048,256]{1,2,0:T(8,128)(2,1)}, u32[]{:S(2)}, u32[]{:S(2)}) async-start(bf16[4,2048,256]{1,2,0:T(8,128)(2,1)} %copy.20), calls=%async_computation | async-start | bytes 8388608 | tf_op jit(solution)/shard_map/all_to_all | solution.py:61
  113.8 0.0 all-gather.4.cloned.1.call-start
  113.9 0.7 all-gather.4.cloned.1.call-update
  114.6 107.6 %all-gather.1 = bf16[4,1,256]{2,1,0:T(2,128)(2,1)S(1)} all-gather(bf16[1,1,256]{2,1,0:T(2,128)(2,1)S(1)} %reshape.292), channel_id=2, replica_groups=mesh['dom'=8,'col'=4] {'col'}, dimensions={0}, use_global_device_ids=true | all-gather | bytes 2560 | tf_op jit(solution)/shard_map/all_gather | solution.py:64
  222.1 19.8 %all-to-all-done = bf16[4,2048,256]{1,2,0:T(8,128)(2,1)} async-done(((bf16[4,2048,256]{1,2,0:T(8,128)(2,1)}), bf16[4,2048,256]{1,2,0:T(8,128)(2,1)}, u32[]{:S(2)}, u32[]{:S(2)}) %all-to-all-start) | async-done | bytes 4194336 | tf_op jit(solution)/shard_map/all_to_all | solution.py:61
  242.0 7.8 %multiply_reduce_fusion.1 = (f32[2048]{0:T(1024)S(1)}, f32[2048,1024]{0,1:T(8,128)S(1)}) fusion(f32[1024]{0:T(1024)S(1)} %bitcast.81, bf16[2048,1024]{0,1:T(8,128)(2,1)} %bitcast.29, bf16[1024,1024]{1,0:T(8,128)(2,1)} %all-gather.4.cloned.1.call-done), kind=kOutput, calls=%fused_computation.11 | convolution fusion | flops 4303353856 | bytes 14692352 | tf_op jit(solution)/shard_map/dot_general | solution.py:66
  249.8 3.5 fusion.6
  253.2 4.8 %all-to-all-start.1 = ((bf16[2048,4,256]{0,2,1:T(8,128)(2,1)}), bf16[2048,4,256]{0,2,1:T(8,128)(2,1)}, u32[]{:S(2)}, u32[]{:S(2)}) async-start(bf16[2048,4,256]{0,2,1:T(8,128)(2,1)} %bitcast.76), calls=%async_computation.1 | async-start | bytes 8388608 | tf_op jit(solution)/shard_map/all_to_all | solution.py:75
  258.1 113.0 %all-reduce = (f32[1024]{0:T(1024)S(1)}, f32[1024]{0:T(1024)S(1)}) all-reduce(f32[1024]{0:T(1024)S(1)} %get-tuple-element.3, f32[1024]{0:T(1024)S(1)} %get-tuple-element.2), channel_id=1, replica_groups=mesh['dom'=8,'col'=4] {'dom','col'}, use_global_device_ids=true, to_apply=%region_4.5 | all-reduce | flops 2048 | bytes 16384 | tf_op jit(solution)/shard_map/psum | solution.py:72
  371.2 0.1 dynamic-slice_multiply_fusion
  371.2 0.6 pad_maximum_fusion
  371.8 0.0 all-to-all-done.1
  371.8 6.2 %copy.21 = bf16[4,2048,256]{2,1,0:T(8,128)(2,1)} copy(bf16[4,2048,256]{1,2,0:T(8,128)(2,1)} %bitcast.32) | data formatting | bytes 8388608 | tf_op jit(solution)/shard_map/all_to_all | solution.py:75
  (29 shorter events, 0.2 us)
Async XLA Ops:
  27.4 9.3 %copy-start.2 = (s32[1,64,4]{1,2,0:T(4,128)S(1)}, s32[1,64,4]{1,2,0:T(4,128)}, u32[]{:S(2)}) copy-start(s32[1,64,4]{1,2,0:T(4,128)} %param.14) | copy-start | bytes 3076
  27.4 9.5 %copy-start.3 = (s32[1,64,4]{1,2,0:T(4,128)S(1)}, s32[1,64,4]{1,2,0:T(4,128)}, u32[]{:S(2)}) copy-start(s32[1,64,4]{1,2,0:T(4,128)} %param.17) | copy-start | bytes 3076
  27.4 9.7 %copy-start.4 = (s32[1,64]{1,0:T(1,128)S(1)}, s32[1,64]{1,0:T(1,128)}, u32[]{:S(2)}) copy-start(s32[1,64]{1,0:T(1,128)} %param.18) | copy-start | bytes 772
  27.4 9.8 %copy-start.5 = (s32[1,64]{1,0:T(1,128)S(1)}, s32[1,64]{1,0:T(1,128)}, u32[]{:S(2)}) copy-start(s32[1,64]{1,0:T(1,128)} %param.15) | copy-start | bytes 772
  30.7 19.4 %collective-permute-start = (bf16[1,512,256]{2,1,0:T(8,128)(2,1)}, bf16[1,512,256]{2,1,0:T(8,128)(2,1)S(1)}, u32[]{:S(2)}, u32[]{:S(2)}) collective-permute-start(bf16[1,512,256]{2,1,0:T(8,128)(2,1)} %get-tuple-element.13), channel_id=1, source_target_pairs={{0,4},{4,8},{8,12},{12,16},{16,20},{20,24},{24,28},{28,0},{1,5},{5... | collective-permute-start | bytes 786440 | tf_op jit(solution)/shard_map/ppermute | solution.py:52
  31.2 20.4 %collective-permute-start.1 = (bf16[1,512,256]{2,1,0:T(8,128)(2,1)}, bf16[1,512,256]{2,1,0:T(8,128)(2,1)S(1)}, u32[]{:S(2)}, u32[]{:S(2)}) collective-permute-start(bf16[1,512,256]{2,1,0:T(8,128)(2,1)} %get-tuple-element.12), channel_id=1, source_target_pairs={{0,8},{4,12},{8,16},{12,20},{16,24},{20,28},{24,0},{28,4},{1,9},{5... | collective-permute-start | bytes 786440 | tf_op jit(solution)/shard_map/ppermute | solution.py:52
  33.7 20.4 %collective-permute-start.2 = (bf16[1,512,256]{2,1,0:T(8,128)(2,1)}, bf16[1,512,256]{2,1,0:T(8,128)(2,1)S(1)}, u32[]{:S(2)}, u32[]{:S(2)}) collective-permute-start(bf16[1,512,256]{2,1,0:T(8,128)(2,1)} %get-tuple-element.11), channel_id=1, source_target_pairs={{0,12},{4,16},{8,20},{12,24},{16,28},{20,0},{24,4},{28,8},{1,13},{... | collective-permute-start | bytes 786440 | tf_op jit(solution)/shard_map/ppermute | solution.py:52
  36.1 18.0 %collective-permute-start.3 = (bf16[1,512,256]{2,1,0:T(8,128)(2,1)}, bf16[1,512,256]{2,1,0:T(8,128)(2,1)S(1)}, u32[]{:S(2)}, u32[]{:S(2)}) collective-permute-start(bf16[1,512,256]{2,1,0:T(8,128)(2,1)} %get-tuple-element.10), channel_id=1, source_target_pairs={{0,16},{4,20},{8,24},{12,28},{16,0},{20,4},{24,8},{28,12},{1,17},{... | collective-permute-start | bytes 786440 | tf_op jit(solution)/shard_map/ppermute | solution.py:52
  36.6 21.3 %collective-permute-start.4 = (bf16[1,512,256]{2,1,0:T(8,128)(2,1)}, bf16[1,512,256]{2,1,0:T(8,128)(2,1)S(1)}, u32[]{:S(2)}, u32[]{:S(2)}) collective-permute-start(bf16[1,512,256]{2,1,0:T(8,128)(2,1)} %get-tuple-element.9), channel_id=1, source_target_pairs={{0,20},{4,24},{8,28},{12,0},{16,4},{20,8},{24,12},{28,16},{1,21},{... | collective-permute-start | bytes 786440 | tf_op jit(solution)/shard_map/ppermute | solution.py:52
  38.0 13.6 %copy-start = (bf16[8,1,512,256]{3,2,1,0:T(8,128)(2,1)S(1)}, bf16[8,1,512,256]{3,2,1,0:T(8,128)(2,1)}, u32[]{:S(2)}) copy-start(bf16[8,1,512,256]{3,2,1,0:T(8,128)(2,1)} %bitcast_dynamic-update-slice_fusion.7) | copy-start | bytes 6291460
  50.1 9.1 %collective-permute-start.5 = (bf16[1,512,256]{2,1,0:T(8,128)(2,1)}, bf16[1,512,256]{2,1,0:T(8,128)(2,1)S(1)}, u32[]{:S(2)}, u32[]{:S(2)}) collective-permute-start(bf16[1,512,256]{2,1,0:T(8,128)(2,1)} %get-tuple-element.8), channel_id=1, source_target_pairs={{0,24},{4,28},{8,0},{12,4},{16,8},{20,12},{24,16},{28,20},{1,25},{... | collective-permute-start | bytes 786440 | tf_op jit(solution)/shard_map/ppermute | solution.py:52
  51.6 9.8 %collective-permute-start.6 = (bf16[1,512,256]{2,1,0:T(8,128)(2,1)}, bf16[1,512,256]{2,1,0:T(8,128)(2,1)S(1)}, u32[]{:S(2)}, u32[]{:S(2)}) collective-permute-start(bf16[1,512,256]{2,1,0:T(8,128)(2,1)} %get-tuple-element.7), channel_id=1, source_target_pairs={{0,28},{4,0},{8,4},{12,8},{16,12},{20,16},{24,20},{28,24},{1,29},{... | collective-permute-start | bytes 786440 | tf_op jit(solution)/shard_map/ppermute | solution.py:52
  61.4 1.3 copy-start.1
  108.8 5.7 %copy-start.6 = (bf16[256]{0:T(256)(128)(2,1)S(1)}, bf16[256]{0:T(256)(128)(2,1)}, u32[]{:S(2)}) copy-start(bf16[256]{0:T(256)(128)(2,1)} %param.13) | copy-start | bytes 1540
  108.8 133.1 %all-to-all-start = ((bf16[4,2048,256]{1,2,0:T(8,128)(2,1)}), bf16[4,2048,256]{1,2,0:T(8,128)(2,1)}, u32[]{:S(2)}, u32[]{:S(2)}) async-start(bf16[4,2048,256]{1,2,0:T(8,128)(2,1)} %copy.20), calls=%async_computation | async-start | bytes 8388608 | tf_op jit(solution)/shard_map/all_to_all | solution.py:61
  113.8 108.3 %all-gather.4.cloned.1.call-start = ((), (), s32[]{:S(2)}) async-start(), calls=%async_computation.2 | async-start | bytes 2621440 | tf_op jit(solution)/shard_map/all_gather | solution.py:63
  253.2 118.6 %all-to-all-start.1 = ((bf16[2048,4,256]{0,2,1:T(8,128)(2,1)}), bf16[2048,4,256]{0,2,1:T(8,128)(2,1)}, u32[]{:S(2)}, u32[]{:S(2)}) async-start(bf16[2048,4,256]{0,2,1:T(8,128)(2,1)} %bitcast.76), calls=%async_computation.1 | async-start | bytes 8388608 | tf_op jit(solution)/shard_map/all_to_all | solution.py:75
Sparse Core Ops, SparseCore 0:
  116.2 99.3 all-gather.3
